TPU v7x, 32 devices: a whole 2x2x4 slice. The times are simulated.
32 devices in a mesh: gx: 2 (over y), gy: 16 (over z, x, core).
Axes of the slice: x: 2, y: 2, z: 4, core: 2. Of those that a mesh axis runs over, the one named last changes fastest.
Arguments:
- basis_mats: float32 [12, 275, 275], replicated, may hold values from -8 to 8.5, as said below
- coeffs: float32 [512, 12], P(('gx', 'gy')), may hold values from 0.5 to 2
- element_loads: float32 [512, 275], P(('gx', 'gy')), may hold values from -18 to 18
- elem_faces: int32 [512, 6], P(('gx', 'gy')), may hold values from 0 to 71, as said below
- orient_codes: int32 [512, 6], P(('gx', 'gy')), may hold values from 0 to 7
- shared_owned: int32 [32, 2, 4], P(('gx', 'gy')), may hold values from 0 to 63, as said below
- shared_remote: int32 [32, 2, 4], P(('gx', 'gy')), may hold values from 0 to 7, as said below
- lower_peers: int32 [32, 2], P(('gx', 'gy')), may hold values from 0 to 31, as said below
- upper_peers: int32 [32, 2], P(('gx', 'gy')), may hold values from 0 to 31, as said below
Outputs:
- trace: float32 [25, 2048], P(None, ('gx', 'gy'))
- residual: float32 [25, 2048], P(None, ('gx', 'gy'))
Inputs may be any that keep to these rules, and one draw needn't show every extreme that they name: `basis_mats`: each matrix is symmetric with every eigenvalue at least 0.5. `elem_faces`: an entry below 64 is a face slot that the element's device owns; an entry 64 + r is that device's remote slot r. Every owned slot of a device is named by one or two of its element faces, every remote slot by exactly one. `shared_owned`: row (d, i) lists 4 distinct owned slots of device d, in message order, that device lower_peers[d, i] uses; the two rows of a device are disjoint. `shared_remote`: row (d, i) lists remote slots of device d in message order: its k-th entry is the face that device upper_peers[d, i] lists k-th in its row i of shared_owned. The two rows of a device together hold each of its 8 remote slots once. upper_peers[lower_peers[d, i], i] = d for every device d and i; the two entries of a row differ. Peers are arbitrary device numbers. lower_peers[upper_peers[d, i], i] = d for every device d and i; the two entries of a row differ; each column is a permutation of the devices. Peers are arbitrary device numbers.
All inputs are finite; a program needn't handle non-finite values.
Results may differ from a plain program's by a relative error of at most 0.0003.
Values sent between devices are 32-bit elements; how exact they have to be, the bound alone decides.
A program may use at most 128 MiB of HBM per device.

v0:
```python
import math

import jax
import jax.numpy as jnp
import numpy as np
from jax import lax
from jax.sharding import PartitionSpec as P

SIDE = 5
FACE_DOFS = 25
CELL_DOFS = 125
TRACE_DOFS = 150
ITERS = 4
FACE_DEV = 64
SHARED = 4
REMOTE = 8


full_precision = lax.Precision.HIGHEST


def orient_table():
    edge_nodes = SIDE
    codes_table = np.zeros((8, edge_nodes * edge_nodes), np.int32)
    for code_index in range(8):
        for first_axis in range(edge_nodes):
            for second_axis in range(edge_nodes):
                if code_index & 1:
                    first_new, second_new = (second_axis, first_axis)
                else:
                    first_new, second_new = (first_axis, second_axis)
                if code_index & 2:
                    first_new = edge_nodes - 1 - first_new
                if code_index & 4:
                    second_new = edge_nodes - 1 - second_new
                codes_table[code_index, first_axis * edge_nodes + second_axis] = (
                    first_new * edge_nodes + second_new
                )
    return codes_table


def permute_mats():
    codes_table = orient_table()
    matrices = np.zeros((8, FACE_DOFS, FACE_DOFS), np.float32)
    for code_index in range(8):
        for position in range(FACE_DOFS):
            matrices[code_index, position, codes_table[code_index, position]] = 1.0
    return matrices


def condense(coeffs, element_loads, basis_mats):
    element_mats = jnp.einsum("ek,kab->eab", coeffs, basis_mats, precision=full_precision)
    inner_block = element_mats[:, :CELL_DOFS, :CELL_DOFS]
    coupling = element_mats[:, :CELL_DOFS, CELL_DOFS:]
    outer_block = element_mats[:, CELL_DOFS:, CELL_DOFS:]
    factor = jnp.linalg.cholesky(inner_block)
    solved = jax.scipy.linalg.solve_triangular(factor, coupling, lower=True)
    source = jax.scipy.linalg.solve_triangular(
        factor, element_loads[:, :CELL_DOFS, None], lower=True
    )[:, :, 0]
    schur_part = outer_block - jnp.einsum("eib,eic->ebc", solved, solved, precision=full_precision)
    load_trace = element_loads[:, CELL_DOFS:] - jnp.einsum(
        "eib,ei->eb", solved, source, precision=full_precision
    )
    return (schur_part, load_trace)


def condense_blocks(coeffs, element_loads, basis_mats):
    elem_count = coeffs.shape[0]
    block_rows = math.gcd(elem_count, 16)
    grouped = (
        coeffs.reshape(-1, block_rows, coeffs.shape[1]),
        element_loads.reshape(-1, block_rows, element_loads.shape[1]),
    )
    schur_part, load_trace = lax.map(
        lambda pieces: condense(pieces[0], pieces[1], basis_mats), grouped
    )
    return (
        schur_part.reshape(elem_count, TRACE_DOFS, TRACE_DOFS),
        load_trace.reshape(elem_count, TRACE_DOFS),
    )


def pick_columns(fields, columns):
    picked = fields[:, :, columns]
    return jnp.moveaxis(picked, 2, 0).reshape(2, -1)


def place_rows(fields, columns, arrived):
    shaped = jnp.moveaxis(arrived.reshape(2, fields.shape[0], FACE_DOFS, SHARED), 0, 2)
    return fields.at[:, :, columns].add(shaped)


def owned_dot(first, second):
    return jnp.sum(first * second)


def on_device(
    basis_mats,
    coeffs,
    element_loads,
    elem_faces,
    orient_codes,
    shared_owned,
    shared_remote,
    lower_peers,
    upper_peers,
):
    elem_count = coeffs.shape[0]
    extent = FACE_DEV + REMOTE
    size_outer = lax.axis_size("gx")
    size_inner = lax.axis_size("gy")
    devices = size_outer * size_inner
    schur_blocks, load_trace = condense_blocks(coeffs, element_loads, basis_mats)
    choose = (orient_codes[:, :, None] == jnp.arange(8, dtype=jnp.int32)[None, None, :]).astype(
        jnp.float32
    )
    permute = jnp.einsum(
        "ejo,oqp->ejqp", choose, jnp.asarray(permute_mats()), precision=full_precision
    )
    incidence = (
        elem_faces.reshape(-1)[:, None] == jnp.arange(extent, dtype=jnp.int32)[None, :]
    ).astype(jnp.float32)
    owned_lists = shared_owned[0]
    remote_lists = FACE_DEV + shared_remote[0]
    lower_ids = lower_peers[0]
    upper_ids = upper_peers[0]

    def spread(field_values):
        gathered = jnp.dot(incidence, field_values.T, precision=full_precision).reshape(
            elem_count, 6, FACE_DOFS
        )
        return jnp.einsum("ejqp,ejp->ejq", permute, gathered, precision=full_precision).reshape(
            elem_count, TRACE_DOFS
        )

    def collect(element_values):
        shaped = element_values.reshape(elem_count, 6, FACE_DOFS)
        placed = jnp.einsum("ejqp,ejq->ejp", permute, shaped, precision=full_precision)
        return jnp.dot(
            placed.reshape(elem_count * 6, FACE_DOFS).T, incidence, precision=full_precision
        )

    def apply_blocks(field_values):
        return collect(
            jnp.einsum("ekl,el->ek", schur_blocks, spread(field_values), precision=full_precision)
        )

    fields = jnp.stack([collect(load_trace), collect(jnp.diagonal(schur_blocks, axis1=1, axis2=2))])

    def upward_bucket(partial_value):
        outgoing = pick_columns(partial_value, remote_lists)
        bucket = jnp.zeros((devices, outgoing.shape[1]), jnp.float32).at[upper_ids].set(outgoing)
        return bucket.reshape(size_outer, size_inner, -1)

    def upward_settle(partial_value, arrived):
        incoming = arrived.reshape(devices, -1)[lower_ids]
        return place_rows(partial_value[:, :, :FACE_DEV], owned_lists, incoming)

    def downward_bucket(values):
        outgoing = pick_columns(values[None], owned_lists)
        bucket = jnp.zeros((devices, outgoing.shape[1]), jnp.float32).at[lower_ids].set(outgoing)
        return bucket.reshape(size_outer, size_inner, -1)

    def downward_settle(values, arrived):
        incoming = arrived.reshape(devices, -1)[upper_ids]
        remote = place_rows(
            jnp.zeros((1, FACE_DOFS, REMOTE), jnp.float32), shared_remote[0], incoming
        )
        return jnp.concatenate([values, remote[0]], axis=1)

    arrived = lax.all_to_all(
        lax.all_to_all(upward_bucket(fields), "gx", split_axis=0, concat_axis=0, tiled=True),
        "gy",
        split_axis=1,
        concat_axis=1,
        tiled=True,
    )
    settled = upward_settle(fields, arrived)

    def operate(values):
        fetched = lax.all_to_all(
            lax.all_to_all(downward_bucket(values), "gx", split_axis=0, concat_axis=0, tiled=True),
            "gy",
            split_axis=1,
            concat_axis=1,
            tiled=True,
        )
        partial_value = apply_blocks(downward_settle(values, fetched))[None]
        returned = lax.all_to_all(
            lax.all_to_all(
                upward_bucket(partial_value), "gx", split_axis=0, concat_axis=0, tiled=True
            ),
            "gy",
            split_axis=1,
            concat_axis=1,
            tiled=True,
        )
        return upward_settle(partial_value, returned)[0]

    rhs_faces = settled[0]
    diag_faces = settled[1]

    def pair_total(residual, precond, mapped):
        return lax.psum((owned_dot(residual, precond), owned_dot(precond, mapped)), ("gx", "gy"))

    trace = jnp.zeros_like(rhs_faces)
    residual = rhs_faces
    precond = residual / diag_faces
    mapped = operate(precond)
    rz_now, curve_sum = pair_total(residual, precond, mapped)
    step_size = rz_now / curve_sum
    direction = precond
    direction_image = mapped
    for iteration in range(ITERS):
        trace = trace + step_size * direction
        residual = residual - step_size * direction_image
        if iteration + 1 < ITERS:
            precond = residual / diag_faces
            mapped = operate(precond)
            rz_next, curve_sum = pair_total(residual, precond, mapped)
            ratio_next = rz_next / rz_now
            step_size = rz_next / (curve_sum - ratio_next * rz_next / step_size)
            direction = precond + ratio_next * direction
            direction_image = mapped + ratio_next * direction_image
            rz_now = rz_next
    return (trace, residual)


def solution(mesh):
    placed = (
        P(),
        P(("gx", "gy"), None),
        P(("gx", "gy"), None),
        P(("gx", "gy"), None),
        P(("gx", "gy"), None),
        P(("gx", "gy"), None, None),
        P(("gx", "gy"), None, None),
        P(("gx", "gy"), None),
        P(("gx", "gy"), None),
    )
    return jax.shard_map(
        on_device,
        mesh=mesh,
        in_specs=placed,
        out_specs=(P(None, ("gx", "gy")), P(None, ("gx", "gy"))),
        check_vma=False,
    )
```

profile of v0, /device:TPU:0, one launch (start us, length us, event | category | flops | bytes accessed | tf_op | source)
XLA Modules:
  0.0 803.4 jit_solution(2315458276905869473)
XLA Ops:
  1.3 9.7 %fusion = f32[16,275,275]{2,0,1:T(8,128)S(1)} fusion(f32[12,275,275]{2,1,0:T(8,128)} %param.10, f32[16,12]{1,0:T(8,128)S(1)} %copy-done), kind=kOutput, calls=%fused_computation.37 | convolution fusion | flops 174240000 | bytes 8470768 | tf_op jit(solution)/shard_map/while/body/eval_jaxpr/ek,kab->eab/dot_general | solution.py:52
  16.7 183.1 %custom-call.13 = f32[16,125,125]{2,1,0:T(8,128)S(1)} custom-call(f32[16,125,125]{2,1,0:T(8,128)S(1)} %fusion.20), custom_call_target="Cholesky" | custom-call | tf_op jit(solution)/shard_map/while/body/eval_jaxpr/jit(cholesky)/cholesky | solution.py:56
  200.3 153.7 %custom-call.14 = f32[16,1,125,125]{2,3,1,0:T(8,128)S(1)} custom-call(f32[16,1,125,125]{3,2,1,0:T(8,128)S(1)} %select_bitcast_fusion), custom_call_target="InvertDiagBlocksLowerTriangular" | custom-call | tf_op jit(solution)/shard_map/while/body/eval_jaxpr/jit(_solve_triangular)/vmap()/triangular_solve | solution.py:57
  377.3 6.7 copy.285
  405.7 6.4 all-to-all-start.1
  412.2 6.5 all-to-all-done.1
  421.7 6.2 all_to_all.90
  432.2 6.3 all-to-all-done.3
  454.3 6.2 all_to_all.91
  464.7 6.4 all-to-all-done.5
  473.1 38.3 %all-reduce.3 = (f32[]{:T(128)}, f32[]{:T(128)}) all-reduce(f32[]{:T(128)} %get-tuple-element.39, f32[]{:T(128)} %get-tuple-element.38), channel_id=1, replica_groups=mesh['gx'=2,'gy'=16] {'gx','gy'}, use_global_device_ids=true, to_apply=%region_5.6 | all-reduce | flops 2 | bytes 16 | tf_op jit(solution)/shard_map/psum | solution.py:205
  514.1 7.4 all_to_all.92
  525.8 6.4 all-to-all-done.7
  558.1 6.4 all-to-all-done.9
  566.5 38.3 %all-reduce.2 = (f32[]{:T(128)}, f32[]{:T(128)}) all-reduce(f32[]{:T(128)} %get-tuple-element.37, f32[]{:T(128)} %get-tuple-element.36), channel_id=1, replica_groups=mesh['gx'=2,'gy'=16] {'gx','gy'}, use_global_device_ids=true, to_apply=%region_13.14 | all-reduce | flops 2 | bytes 16 | tf_op jit(solution)/shard_map/psum | solution.py:205
  610.7 7.4 all_to_all.94
  622.4 6.4 all-to-all-done.11
  654.8 6.4 all-to-all-done.13
  663.2 38.3 %all-reduce.1 = (f32[]{:T(128)}, f32[]{:T(128)}) all-reduce(f32[]{:T(128)} %get-tuple-element.35, f32[]{:T(128)} %get-tuple-element.34), channel_id=1, replica_groups=mesh['gx'=2,'gy'=16] {'gx','gy'}, use_global_device_ids=true, to_apply=%region_21.22 | all-reduce | flops 2 | bytes 16 | tf_op jit(solution)/shard_map/psum | solution.py:205
  706.9 7.4 all_to_all.96
  718.6 6.4 all-to-all-done.15
  740.6 6.2 all_to_all.97
  751.0 6.4 all-to-all-done.17
  759.5 38.4 %all-reduce = (f32[]{:T(128)}, f32[]{:T(128)}) all-reduce(f32[]{:T(128)} %get-tuple-element.33, f32[]{:T(128)} %get-tuple-element.32), channel_id=1, replica_groups=mesh['gx'=2,'gy'=16] {'gx','gy'}, use_global_device_ids=true, to_apply=%region_29.30 | all-reduce | flops 2 | bytes 16 | tf_op jit(solution)/shard_map/psum | solution.py:205
  (255 shorter events, 176.7 us)
Async XLA Ops:
  0.6 0.7 copy-start
  11.1 2.8 copy-start.2
  354.0 5.9 slice-start
  360.9 5.6 copy-start.4
  360.9 5.9 copy-start.3
  360.9 5.9 copy-start.5
  370.6 2.7 copy-start.1
  370.6 2.6 copy-start.6
  384.0 10.8 %copy-start.7 = (s32[1,2,4]{2,1,0:T(2,128)S(1)}, s32[1,2,4]{2,1,0:T(2,128)}, u32[]{:S(2)}) copy-start(s32[1,2,4]{2,1,0:T(2,128)} %param.16) | copy-start | bytes 100
  384.0 11.7 %copy-start.9 = (s32[1,2]{1,0:T(1,128)S(1)}, s32[1,2]{1,0:T(1,128)}, u32[]{:S(2)}) copy-start(s32[1,2]{1,0:T(1,128)} %param.18) | copy-start | bytes 28
  384.0 17.1 %copy-start.10 = (s32[1,2]{1,0:T(1,128)S(1)}, s32[1,2]{1,0:T(1,128)}, u32[]{:S(2)}) copy-start(s32[1,2]{1,0:T(1,128)} %param.17) | copy-start | bytes 28
  384.0 17.1 %copy-start.8 = (s32[1,2,4]{2,1,0:T(2,128)S(1)}, s32[1,2,4]{2,1,0:T(2,128)}, u32[]{:S(2)}) copy-start(s32[1,2,4]{2,1,0:T(2,128)} %param.15) | copy-start | bytes 100
  396.9 8.2 %all-to-all-start = ((f32[2,16,200]{2,1,0:T(8,128)}), f32[2,16,200]{2,1,0:T(8,128)S(1)}, u32[]{:S(2)}, u32[]{:S(2)}) async-start(f32[2,16,200]{2,1,0:T(8,128)} %bitcast.26), calls=%async_computation | async-start | bytes 65536 | tf_op jit(solution)/shard_map/all_to_all | solution.py:173
  405.7 13.0 %all-to-all-start.1 = ((f32[2,16,200]{2,0,1:T(2,128)}), f32[2,16,200]{2,0,1:T(2,128)S(1)}, u32[]{:S(2)}, u32[]{:S(2)}) async-start(f32[2,16,200]{2,0,1:T(2,128)} %copy.290), calls=%async_computation.1 | async-start | bytes 65536 | tf_op jit(solution)/shard_map/all_to_all | solution.py:172
  428.6 10.0 %all-to-all-start.3 = ((f32[2,16,100]{2,0,1:T(2,128)}), f32[2,16,100]{2,0,1:T(2,128)S(1)}, u32[]{:S(2)}, u32[]{:S(2)}) async-start(f32[2,16,100]{2,0,1:T(2,128)} %copy.298), calls=%async_computation.3 | async-start | bytes 32768 | tf_op jit(solution)/shard_map/all_to_all | solution.py:182
  461.1 10.0 %all-to-all-start.5 = ((f32[2,16,100]{2,0,1:T(2,128)}), f32[2,16,100]{2,0,1:T(2,128)S(1)}, u32[]{:S(2)}, u32[]{:S(2)}) async-start(f32[2,16,100]{2,0,1:T(2,128)} %copy.306), calls=%async_computation.5 | async-start | bytes 32768 | tf_op jit(solution)/shard_map/all_to_all | solution.py:190
  522.1 10.1 %all-to-all-start.7 = ((f32[2,16,100]{2,0,1:T(2,128)}), f32[2,16,100]{2,0,1:T(2,128)S(1)}, u32[]{:S(2)}, u32[]{:S(2)}) async-start(f32[2,16,100]{2,0,1:T(2,128)} %copy.312), calls=%async_computation.7 | async-start | bytes 32768 | tf_op jit(solution)/shard_map/all_to_all | solution.py:182
  554.5 10.0 %all-to-all-start.9 = ((f32[2,16,100]{2,0,1:T(2,128)}), f32[2,16,100]{2,0,1:T(2,128)S(1)}, u32[]{:S(2)}, u32[]{:S(2)}) async-start(f32[2,16,100]{2,0,1:T(2,128)} %copy.320), calls=%async_computation.9 | async-start | bytes 32768 | tf_op jit(solution)/shard_map/all_to_all | solution.py:190
  618.8 10.0 %all-to-all-start.11 = ((f32[2,16,100]{2,0,1:T(2,128)}), f32[2,16,100]{2,0,1:T(2,128)S(1)}, u32[]{:S(2)}, u32[]{:S(2)}) async-start(f32[2,16,100]{2,0,1:T(2,128)} %copy.326), calls=%async_computation.11 | async-start | bytes 32768 | tf_op jit(solution)/shard_map/all_to_all | solution.py:182
  651.2 10.0 %all-to-all-start.13 = ((f32[2,16,100]{2,0,1:T(2,128)}), f32[2,16,100]{2,0,1:T(2,128)S(1)}, u32[]{:S(2)}, u32[]{:S(2)}) async-start(f32[2,16,100]{2,0,1:T(2,128)} %copy.334), calls=%async_computation.13 | async-start | bytes 32768 | tf_op jit(solution)/shard_map/all_to_all | solution.py:190
  714.9 10.1 %all-to-all-start.15 = ((f32[2,16,100]{2,0,1:T(2,128)}), f32[2,16,100]{2,0,1:T(2,128)S(1)}, u32[]{:S(2)}, u32[]{:S(2)}) async-start(f32[2,16,100]{2,0,1:T(2,128)} %copy.340), calls=%async_computation.15 | async-start | bytes 32768 | tf_op jit(solution)/shard_map/all_to_all | solution.py:182
  747.4 10.0 %all-to-all-start.17 = ((f32[2,16,100]{2,0,1:T(2,128)}), f32[2,16,100]{2,0,1:T(2,128)S(1)}, u32[]{:S(2)}, u32[]{:S(2)}) async-start(f32[2,16,100]{2,0,1:T(2,128)} %copy.348), calls=%async_computation.17 | async-start | bytes 32768 | tf_op jit(solution)/shard_map/all_to_all | solution.py:190
where the time goes:
time: 814 us; the launch traced here: 803 us
  other arithmetic  351 us (43%)
  blocking collectives  207 us (25%)
  matrix products  79.3 us (10%)
  waiting for transfers between devices  61.3 us (8%)
  local copies, waits for them, and re-layouts  50.7 us (6%)
  starting transfers between devices  38.8 us (5%)
  between operations  15.4 us (2%)
    another operation x4, other arithmetic, condense(): factor = jnp.linalg.cholesky(inner_block)  183 us
    another operation x3, other arithmetic, condense(): solved = jax.scipy.linalg.solve_triangular(factor, coupling, lower=True)  154 us
    psum x4, blocking collectives, pair_total(): lax.psum((owned_dot(residual, precond), owned_dot(precond, mapped)), ('gx...  153 us
    all_to_all x4, blocking collectives, operate(): lax.all_to_all(downward_bucket(values), 'gx', split_axis=0, concat_axis=0...  28.4 us
    all_to_all x4, waiting for transfers between devices, operate(): lax.all_to_all(lax.all_to_all(downward_bucket(values), 'gx', split_axis=0...  25.5 us
    all_to_all x4, waiting for transfers between devices, operate(): lax.all_to_all(lax.all_to_all(upward_bucket(partial_value), 'gx', split_a...  25.4 us
    all_to_all x4, blocking collectives, operate(): lax.all_to_all(upward_bucket(partial_value), 'gx', split_axis=0, concat_a...  24.8 us
    dot_general x6, matrix products, collect(): jnp.einsum('ejqp,ejq->ejp', permute, shaped, precision=full_precision)  22.3 us
  transfers between devices with their start and end apart: 10, of which 10 were waited for; matrix products, arithmetic and copies ran while one was open for 0% of the time, Pallas kernels for 0%

commit v1 on v0

v1 whole, which is shorter than its diff:
```python
import functools

import jax
import jax.numpy as jnp
import numpy as np
from jax import lax
from jax.experimental import pallas as pl
from jax.experimental.pallas import tpu as pltpu
from jax.sharding import PartitionSpec as P

SIDE = 5
FACE_DOFS = 25
CELL_DOFS = 125
TRACE_DOFS = 150
LOCAL_DOFS = 275
ITERS = 4
FACE_DEV = 64
SHARED = 4
REMOTE = 8
LANES = 128
ROWS = 160
NB = 32
BF = jnp.bfloat16
F32 = jnp.float32


def orient_table():
    n = SIDE
    table = np.zeros((8, n * n), np.int32)
    for code in range(8):
        for a in range(n):
            for b in range(n):
                a2, b2 = (b, a) if code & 1 else (a, b)
                if code & 2:
                    a2 = n - 1 - a2
                if code & 4:
                    b2 = n - 1 - b2
                table[code, a * n + b] = a2 * n + b2
    return table


def permute_stack():
    table = orient_table()
    out = np.zeros((32, 256), np.float32)
    for code in range(8):
        for q in range(FACE_DOFS):
            out[q, 32 * code + table[code, q]] = 1.0
    return out


def iota(shape, dim):
    return lax.broadcasted_iota(jnp.int32, shape, dim)


def hi_part(x):
    return x.astype(BF).astype(F32)


def pack_lanes(x, source):
    lane = iota(x.shape, 1)

    def at(place):
        shift = (place - source) % LANES
        return x if shift == 0 else pltpu.roll(x, shift, 1)

    x0, x1, x2 = at(0), at(NB), at(2 * NB)
    packed = jnp.where(lane < NB, x0, jnp.where(lane < 2 * NB, x1 - hi_part(x1), x2))
    return jnp.where(lane < 3 * NB, packed, 0.0).astype(BF)


def pack_rows(x):
    high = x.astype(BF)
    low = (x - high.astype(F32)).astype(BF)
    return jnp.concatenate([high, high, low, jnp.zeros_like(high)], axis=0)


def invert_blocks(tiles):
    lane = iota((8, LANES), 1)
    sub = iota((8, LANES), 0)
    inside = lane % NB
    first = lane - inside
    for k in range(NB):
        tk, sk = k // 8, k % 8
        pick = first + k
        here = inside == k
        for g in range(len(tiles)):
            group = tiles[g]
            row = jnp.broadcast_to(group[tk][sk : sk + 1, :], (8, LANES))
            pivot = jnp.take_along_axis(row, pick, axis=1)
            inverse = 1.0 / pivot
            new_row = jnp.where(here, inverse, row * inverse)
            fresh = []
            for t in range(4):
                column = jnp.take_along_axis(group[t], pick, axis=1)
                value = jnp.where(here, 0.0, group[t]) - column * new_row
                if t == tk:
                    value = jnp.where(sub == sk, new_row, value)
                fresh.append(value)
            tiles[g] = fresh
    return tiles


def condense_kernel(elems, terms, coef_ref, basis_ref, load_ref, shi_ref, slo_ref, diag_ref, lrow_ref, x_ref, d_ref):
    lane8 = iota((8, LANES), 1)
    sub8 = iota((8, LANES), 0)
    tail = LOCAL_DOFS - 256

    def combine(row_slice, count, emit):
        parts = [
            [basis_ref[k, row_slice, 0:128], basis_ref[k, row_slice, 128:256], basis_ref[k, row_slice, 256:LOCAL_DOFS]]
            for k in range(terms)
        ]
        for e in range(elems):
            total = None
            for k in range(terms):
                scaled = [coef_ref[e, k] * part for part in parts[k]]
                total = scaled if total is None else [a + b for a, b in zip(total, scaled)]
            t0, t1, t2 = total
            t2 = jnp.concatenate([t2, jnp.zeros((count, LANES - tail), F32)], axis=1)
            if count < 8:
                t0, t1, t2 = (
                    jnp.concatenate([t, jnp.zeros((8 - count, LANES), F32)], axis=0) for t in (t0, t1, t2)
                )
            emit(e, t0, t1, t2)

    def put_inner(e, start, t0, t1, t2, edge):
        inner = lane8 < CELL_DOFS
        moved = jnp.where(inner, t2, t0)
        kept = jnp.where(inner, t0, 0.0)
        if edge:
            good = sub8 + 120 < CELL_DOFS
            kept = jnp.where(good, kept, jnp.where(sub8 + 120 == lane8, 1.0, 0.0))
            t1 = jnp.where(good, t1, 0.0)
            moved = jnp.where(good, moved, 0.0)
        x_ref[e, pl.ds(start, 8), 0:128] = kept
        x_ref[e, pl.ds(start, 8), 128:256] = t1
        x_ref[e, pl.ds(start, 8), 256:384] = moved

    def put_outer(e, start, t0, t1, t2):
        inner = lane8 < CELL_DOFS
        x_ref[e, pl.ds(start, 8), 0:128] = jnp.where(inner, t0, 0.0)
        x_ref[e, pl.ds(start, 8), 128:256] = t1
        x_ref[e, pl.ds(start, 8), 256:384] = jnp.where(inner, t2, t0)

    @pl.loop(0, 15)
    def _(t):
        start = pl.multiple_of(t * 8, 8)
        combine(pl.ds(start, 8), 8, lambda e, a, b, c: put_inner(e, start, a, b, c, False))

    def edge_rows(e, t0, t1, t2):
        put_inner(e, 120, t0, t1, t2, True)
        first = sub8 == 0

        def with_load(tile, lo):
            return jnp.where(first, jnp.broadcast_to(load_ref[e : e + 1, lo : lo + 128], (8, LANES)), tile)

        put_outer(e, 128, with_load(t0, 0), with_load(t1, 128), with_load(t2, 256))

    combine(pl.ds(120, 8), 8, edge_rows)

    @pl.loop(16, 34)
    def _(t):
        start = pl.multiple_of(t * 8, 8)
        combine(pl.ds(start, 8), 8, lambda e, a, b, c: put_outer(e, start + 8, a, b, c))

    combine(pl.ds(272, 3), 3, lambda e, a, b, c: put_outer(e, 280, a, b, c))

    groups = elems // 4
    lane32 = iota((NB, LANES), 1)
    for b in range(4):
        rows = slice(NB * b, NB * b + NB)
        tiles = []
        for g in range(groups):
            whole = jnp.zeros((NB, LANES), F32)
            for q in range(4):
                part = x_ref[g * 4 + q, rows, 0:128]
                shift = (NB * (q - b)) % LANES
                if shift:
                    part = pltpu.roll(part, shift, 1)
                whole = jnp.where(lane32 // NB == q, part, whole)
            tiles.append([whole[8 * t : 8 * t + 8] for t in range(4)])
        tiles = invert_blocks(tiles)
        for g in range(groups):
            whole = jnp.concatenate(tiles[g], axis=0)
            for q in range(4):
                d_ref[g * 4 + q] = pack_lanes(whole, NB * q)
        lo = 0 if b < 3 else LANES

        @pl.loop(0, elems)
        def _(e):
            scaled = jnp.dot(d_ref[e], pack_rows(x_ref[e, rows, lo:384]), preferred_element_type=F32)
            lhs = pack_lanes(x_ref[e, NB * (b + 1) : 288, 0:128], NB * b)
            update = jnp.dot(lhs, pack_rows(scaled), preferred_element_type=F32)
            x_ref[e, NB * (b + 1) : 288, lo:384] = x_ref[e, NB * (b + 1) : 288, lo:384] - update

    diag_ref[...] = jnp.zeros_like(diag_ref)
    lane_w = iota((ROWS, 256), 1)
    on_diag = (iota((ROWS, 256), 0) + 248) % 256 == lane_w
    lane_t = iota((ROWS, LANES), 1)

    @pl.loop(0, elems)
    def _(e):
        s = x_ref[e, 128:288, 128:384]
        high = s.astype(BF)
        start = pl.multiple_of(e * ROWS, 32)
        shi_ref[pl.ds(start, ROWS), :] = high
        slo_ref[pl.ds(start, ROWS), :] = (s - high.astype(F32)).astype(BF)
        only = jnp.where(on_diag, s, 0.0)
        column = jnp.sum(only[:, 0:128] + only[:, 128:256], axis=1, keepdims=True)
        diag_ref[...] = jnp.where(lane_t == e, column, diag_ref[...])
        lrow_ref[pl.ds(e, 1), :] = s[0:1, :]


def split3(x):
    a = x.astype(BF)
    rest = x - a.astype(F32)
    b = rest.astype(BF)
    c = (rest - b.astype(F32)).astype(BF)
    return a, b, c


def cg_kernel(
    mesh_names, sizes, elems, upper_ref, lower_ref, ints_ref, perm_ref, permt_ref, shi_ref, slo_ref, diag_ref, lrow_ref,
    trace_ref, resid_ref, buf_refs, send_ref, send_sem, recv_sem,
):
    devices = sizes[0] * sizes[1]
    me = lax.axis_index(mesh_names[0]) * sizes[1] + lax.axis_index(mesh_names[1])

    def coords(d):
        return (d // sizes[1], lax.rem(d, sizes[1]))

    barrier = pltpu.get_barrier_semaphore()

    def greet(k, carry):
        pl.semaphore_signal(
            barrier, inc=1, device_id=coords(lax.rem(me + k, devices)), device_id_type=pl.DeviceIdType.MESH
        )
        return carry

    lax.fori_loop(1, devices, greet, 0)

    square = (LANES, LANES)
    sub = iota(square, 0)
    inc_t = jnp.where(sub == ints_ref[0:1, :], 1.0, 0.0)
    inc = inc_t.T
    sel = jnp.where(sub == ints_ref[2:3, :], 1.0, 0.0).astype(BF)
    place = jnp.where(sub == ints_ref[3:4, :], 1.0, 0.0).T.astype(BF)
    inc_t = inc_t.astype(BF)
    inc = inc.astype(BF)
    inc_sel = jnp.dot(inc, sel, preferred_element_type=F32).astype(BF)
    out_mat = jnp.concatenate([inc, inc_sel], axis=1)
    perm = perm_ref[...]
    perm_t = permt_ref[...]
    code = ints_ref[1:2, :]
    lane32 = iota((32, LANES), 1)
    sub32 = iota((32, LANES), 0)
    in_group = lane32 // 16 == sub32 // 4
    lane4 = iota((4, LANES), 1)
    slot4 = lane4 % 16
    owned = lane32 < FACE_DEV

    def spread(field):
        a, b, c = split3(field)
        got = jnp.dot(jnp.concatenate([a, b, c], axis=0), inc_t, preferred_element_type=F32)
        pieces = []
        for s in range(3):
            part = got[32 * s : 32 * s + 32]
            pieces.append(
                jnp.concatenate([jnp.where(code == o, part, 0.0) for o in range(8)], axis=0).astype(BF)
            )
        return jnp.dot(perm, jnp.concatenate(pieces, axis=1), preferred_element_type=F32)

    def columns(values):
        blocks = []
        for j in range(6):
            block = jnp.zeros((32, LANES), F32)
            for s in range(3):
                part = values[:, LANES * s : LANES * s + LANES]
                shift = (16 * s - 16 * j) % LANES
                if shift:
                    part = pltpu.roll(part, shift, 1)
                block = jnp.where(lane32 // 16 == s, part, block)
            blocks.append(block)
        return jnp.concatenate(
            [blocks[0][3:25]] + [x[0:25] for x in blocks[1:]] + [jnp.zeros((106, LANES), F32), blocks[0][0:3]], axis=0
        ).astype(BF)

    def by_face(slices):
        out = jnp.zeros((32, LANES), F32)
        for j in range(6):
            part = jnp.concatenate([slices[j], jnp.zeros((7, LANES), F32)], axis=0)
            if j:
                part = pltpu.roll(part, 16 * j, 1)
            out = jnp.where(lane32 // 16 == j, part, out)
        return out

    def from_rows(t):
        return by_face([t[5 + 25 * j : 30 + 25 * j] for j in range(6)])

    def collect(values):
        turned = jnp.dot(perm_t, jnp.concatenate(split3(values), axis=1), preferred_element_type=F32)
        turned = turned[:, 0:128] + turned[:, 128:256] + turned[:, 256:384]
        placed = jnp.zeros((32, LANES), F32)
        for o in range(8):
            placed = jnp.where(code == o, turned[32 * o : 32 * o + 32], placed)
        both = jnp.dot(jnp.concatenate(split3(placed), axis=0), out_mat, preferred_element_type=F32)
        both = both[0:32] + both[32:64] + both[64:96]
        return both[:, 0:128], both[:, 128:256]

    def pack(message):
        kept = jnp.where(in_group, message, 0.0)
        out = kept[0:4]
        for g in range(1, 8):
            out = out + kept[4 * g : 4 * g + 4]
        return out

    def unpack(message):
        tall = jnp.where(in_group, jnp.concatenate([message] * 8, axis=0), 0.0)
        both = jnp.dot(jnp.concatenate(split3(tall), axis=0), place, preferred_element_type=F32)
        return both[0:32] + both[32:64] + both[64:96]

    def exchange(slot, parts):
        count = len(parts)
        buf_ref = buf_refs[slot]
        own_rows = send_ref.at[slot, 0 : 4 * count]
        for i, part in enumerate(parts):
            send_ref[slot, 4 * i : 4 * i + 4] = part
            buf_ref[me, 4 * i : 4 * i + 4] = part

        def send(k, carry):
            pltpu.make_async_remote_copy(
                src_ref=own_rows,
                dst_ref=buf_ref.at[me],
                send_sem=send_sem.at[slot],
                recv_sem=recv_sem.at[slot],
                device_id=coords(lax.rem(me + k, devices)),
                device_id_type=pl.DeviceIdType.MESH,
            ).start()
            return carry

        lax.fori_loop(1, devices, send, 0)
        every = buf_ref.at[pl.ds(0, devices - 1)]
        pltpu.make_async_copy(every, every, recv_sem.at[slot]).wait()
        pltpu.make_async_copy(every, every, send_sem.at[slot]).wait()
        from_upper = [buf_ref[upper_ref[0, i]] for i in range(2)]
        from_lower = [buf_ref[lower_ref[0, i]] for i in range(2)]
        out = []
        for i in range(count):
            rows = slice(4 * i, 4 * i + 4)
            mixed = jnp.where(
                slot4 < 4,
                from_upper[0][rows],
                jnp.where(
                    slot4 < 8, from_upper[1][rows], jnp.where(slot4 < 12, from_lower[0][rows], from_lower[1][rows])
                ),
            )
            out.append(unpack(mixed))
        return out

    spare = (lane4 // 16 == 6) & (iota((4, LANES), 0) == 1)

    diag_part, diag_out = collect(from_rows(diag_ref[...]))
    padded = jnp.concatenate([lrow_ref[...], jnp.zeros((LANES - elems, 256), F32)], axis=0)
    turned = jnp.concatenate([padded[:, 0:128].T, padded[:, 128:256].T], axis=0)
    slices = [jnp.concatenate([turned[253:256], turned[0:22]], axis=0)]
    slices += [turned[25 * j - 3 : 25 * j + 22] for j in range(1, 6)]
    load_part, load_out = collect(by_face(slices))
    pl.semaphore_wait(barrier, devices - 1)
    got = exchange(0, [pack(load_out), pack(diag_out)])
    live = (lane32 < FACE_DEV + REMOTE) & (sub32 < FACE_DOFS)
    residual = jnp.where(live, load_part + got[0], 0.0)
    weights = jnp.where(live, 1.0 / jnp.where(live, diag_part + got[1], 1.0), 0.0)

    trace = jnp.zeros((32, LANES), F32)
    direction = jnp.zeros((32, LANES), F32)
    image = jnp.zeros((32, LANES), F32)
    rz_now = None
    step = None
    row_lane = iota((ROWS, LANES), 1)
    row_elem = jnp.where(row_lane < 48, row_lane % 16, -1)
    for iteration in range(ITERS):
        precond = residual * weights
        values = spread(precond)
        cols = columns(values)
        total = jnp.zeros((ROWS, LANES), F32)
        for e in range(elems):
            rows = slice(ROWS * e, ROWS * e + ROWS)
            product = jnp.dot(shi_ref[rows], cols, preferred_element_type=F32)
            product = product + jnp.dot(slo_ref[rows], cols, preferred_element_type=F32)
            total = jnp.where(row_elem == e, product, total)
        total = total + pltpu.roll(total, LANES - 16, 1) + pltpu.roll(total, LANES - 32, 1)
        result = from_rows(total)
        flat = values[:, 0:128] + values[:, 128:256] + values[:, 256:384]
        curve_part = jnp.sum(jnp.where(lane32 < 6 * elems, flat * result, 0.0))
        rz_part = jnp.sum(jnp.where(owned, residual * precond, 0.0))
        part, out = collect(result)
        message = pack(out)
        message = jnp.where(spare, jnp.where(slot4 == 0, rz_part, jnp.where(slot4 == 1, curve_part, 0.0)), message)
        slot = iteration + 1
        got = exchange(slot, [message])[0]

        def add(d, carry):
            return carry + buf_refs[slot][d]

        sums = lax.fori_loop(0, devices, add, jnp.zeros((4, LANES), F32))
        rz_next = jnp.sum(jnp.where(spare & (slot4 == 0), sums, 0.0), keepdims=True)
        curve = jnp.sum(jnp.where(spare & (slot4 == 1), sums, 0.0), keepdims=True)
        mapped = jnp.where(live, part + got, 0.0)
        if iteration == 0:
            step = rz_next / curve
            direction, image = precond, mapped
        else:
            ratio = rz_next / rz_now
            step = rz_next / (curve - ratio * rz_next / step)
            direction = precond + ratio * direction
            image = mapped + ratio * image
        rz_now = rz_next
        trace = trace + step * direction
        residual = residual - step * image
    trace_ref[...] = trace[0:FACE_DOFS, 0:FACE_DEV]
    resid_ref[...] = residual[0:FACE_DOFS, 0:FACE_DEV]


def on_device(
    sizes, basis_mats, coeffs, element_loads, elem_faces, orient_codes, shared_owned, shared_remote, lower_peers, upper_peers
):
    elems, terms = coeffs.shape
    vmem = pl.BlockSpec(memory_space=pltpu.VMEM)
    smem = pl.BlockSpec(memory_space=pltpu.SMEM)
    loads = jnp.pad(element_loads, ((0, 0), (0, 384 - LOCAL_DOFS)))
    shi, slo, diag, lrow = pl.pallas_call(
        functools.partial(condense_kernel, elems, terms),
        out_shape=(
            jax.ShapeDtypeStruct((elems * ROWS, 256), BF),
            jax.ShapeDtypeStruct((elems * ROWS, 256), BF),
            jax.ShapeDtypeStruct((ROWS, LANES), F32),
            jax.ShapeDtypeStruct((elems, 256), F32),
        ),
        in_specs=[smem, vmem, vmem],
        out_specs=(vmem, vmem, vmem, vmem),
        scratch_shapes=[pltpu.VMEM((elems, 288, 384), F32), pltpu.VMEM((elems, NB, LANES), BF)],
        compiler_params=pltpu.CompilerParams(vmem_limit_bytes=40 * 1024 * 1024),
        name="condense",
    )(coeffs, basis_mats, loads)

    def lane_row(values, fill):
        flat = values.reshape(1, -1)
        return jnp.pad(flat, ((0, 0), (0, LANES - flat.shape[1])), constant_values=fill)

    own = shared_owned.reshape(-1)
    far = FACE_DEV + shared_remote.reshape(-1)
    ints = jnp.concatenate(
        [
            lane_row(elem_faces.T, -1),
            lane_row(orient_codes.T, 0),
            jnp.tile(jnp.concatenate([own, far]), 8)[None],
            jnp.tile(jnp.concatenate([far, own]), 8)[None],
            jnp.zeros((4, LANES), jnp.int32),
        ],
        axis=0,
    )
    stack = permute_stack()
    devices = sizes[0] * sizes[1]
    return pl.pallas_call(
        functools.partial(cg_kernel, ("gx", "gy"), sizes, elems),
        out_shape=(
            jax.ShapeDtypeStruct((FACE_DOFS, FACE_DEV), F32),
            jax.ShapeDtypeStruct((FACE_DOFS, FACE_DEV), F32),
        ),
        in_specs=[smem, smem] + [vmem] * 7,
        out_specs=(vmem, vmem),
        scratch_shapes=[
            [pltpu.VMEM((devices, 8 if i == 0 else 4, LANES), F32) for i in range(ITERS + 1)],
            pltpu.VMEM((ITERS + 1, 8, LANES), F32),
            pltpu.SemaphoreType.DMA((ITERS + 1,)),
            pltpu.SemaphoreType.DMA((ITERS + 1,)),
        ],
        compiler_params=pltpu.CompilerParams(
            collective_id=0, has_side_effects=True, vmem_limit_bytes=48 * 1024 * 1024
        ),
        name="solve",
    )(
        upper_peers, lower_peers, ints, jnp.asarray(stack, BF), jnp.asarray(stack.T, BF), shi, slo, diag, lrow
    )


def solution(mesh):
    row = P(("gx", "gy"), None)
    cube = P(("gx", "gy"), None, None)
    sizes = (mesh.shape["gx"], mesh.shape["gy"])
    return jax.shard_map(
        functools.partial(on_device, sizes),
        mesh=mesh,
        in_specs=(P(), row, row, row, row, cube, cube, row, row),
        out_specs=(P(None, ("gx", "gy")), P(None, ("gx", "gy"))),
        check_vma=False,
    )
```

time: 814 us -> 90.6 us (0.11); the launches traced: 803 us -> 90.2 us
  other arithmetic: 351 us -> 0.76 us
  blocking collectives: 207 us -> 0 us
  Pallas kernels: 0 us -> 81.1 us
  matrix products: 79.3 us -> 0 us
  waiting for transfers between devices: 61.3 us -> 0 us
  local copies, waits for them, and re-layouts: 50.7 us -> 7.72 us
  starting transfers between devices: 38.8 us -> 0 us
  between operations: 15.4 us -> 0.69 us
    another operation x9 -> x0, other arithmetic: 337 us -> none  [the longest x4 183 us: condense(): factor = jnp.linalg.cholesky(inner_block)]
    psum x4 -> x0, blocking collectives: 153 us -> none  [pair_total(): lax.psum((owned_dot(residual, precond), owned_dot(precond, mapped)), ('gx...]
    pallas_call x0 -> x2, Pallas kernels: none -> 81.1 us  [the longest x1 42 us: on_device(): pl.pallas_call(functools.partial(condense_kernel, elems, terms), out_shap...]
    dot_general x28 -> x0, matrix products: 72.4 us -> none  [the longest x6 22.3 us: collect(): jnp.einsum('ejqp,ejq->ejp', permute, shaped, precision=full_precision)]
    all_to_all x10 -> x0, waiting for transfers between devices: 61.3 us -> none  [the longest x4 25.5 us: operate(): lax.all_to_all(lax.all_to_all(downward_bucket(values), 'gx', split_axis=0...]
    all_to_all x8 -> x0, blocking collectives: 53.2 us -> none  [the longest x4 28.4 us: operate(): lax.all_to_all(downward_bucket(values), 'gx', split_axis=0, concat_axis=0...]
    all_to_all x10 -> x0, starting transfers between devices: 38.8 us -> none  [the longest x4 14.2 us: operate(): lax.all_to_all(lax.all_to_all(downward_bucket(values), 'gx', split_axis=0...]
    gather x29 -> x0, local copies, waits for them, and re-layouts: 16.9 us -> none  [the longest x2 6.01 us: on_device(): jnp.diagonal(schur_blocks, axis1=1, axis2=2)]
  transfers between devices with their start and end apart: 10 -> 0, of which waited for: 10 -> 0; matrix products, arithmetic and copies ran while one was open for 0% -> 0% of each run, Pallas kernels for 0% -> 0%
where the time goes in v1:
time: 90.6 us; the launch traced here: 90.2 us
  Pallas kernels  81.1 us (90%)
  local copies, waits for them, and re-layouts  7.72 us (9%)
    pallas_call x1, Pallas kernels, on_device(): pl.pallas_call(functools.partial(condense_kernel, elems, terms), out_shap...  42 us
    pallas_call x1, Pallas kernels, on_device(): pl.pallas_call(functools.partial(cg_kernel, ('gx', 'gy'), sizes, elems),...  39.1 us
    unnamed x14, local copies, waits for them, and re-layouts  4.39 us

profile of v1, /device:TPU:0, one launch (start us, length us, event | category | flops | bytes accessed | tf_op | source)
XLA Modules:
  0.0 90.2 jit_solution(17991861430429422475)
XLA Ops:
  0.6 0.8 reshape.18
  1.4 0.8 reshape.19
  2.2 0.8 reshape.20
  2.9 0.7 broadcast_add_fusion
  3.6 0.1 add.13
  3.7 0.1 pad_add_fusion.1
  3.8 0.1 broadcast_in_dim_tile.7
  3.9 0.1 broadcast_in_dim_tile.6
  4.0 0.7 pad.13.load_ref
  4.7 0.0 copy-start
  4.7 2.5 %copy-done = f32[12,275,275]{2,1,0:T(8,128)S(1)} copy-done((f32[12,275,275]{2,1,0:T(8,128)S(1)}, f32[12,275,275]{2,1,0:T(8,128)}, u32[]{:S(2)}) %copy-start) | copy-done | bytes 3630024
  7.2 0.0 copy-start.3
  7.2 0.7 copy-done.3
  7.9 0.0 copy-start.1
  7.9 0.0 copy-start.2
  7.9 0.0 copy-start.4
  7.9 42.0 %condense.1 = (bf16[2560,256]{1,0:T(8,128)(2,1)S(1)}, bf16[2560,256]{1,0:T(8,128)(2,1)S(1)}, f32[160,128]{1,0:T(8,128)S(1)}, f32[16,256]{1,0:T(8,128)S(1)}) custom-call(f32[16,12]{1,0:T(8,128)S(1)} %copy-done.3, f32[12,275,275]{2,1,0:T(8,128)S(1)} %copy-done, f32[16,384]{1,0:T(8,128)S(1)} %pad.13.load_ref), custom_call_target="tpu_custom_call" | custom-call | tf_op jit(solution)/shard_map/condense/pallas_call | solution.py:431
  49.9 0.0 copy-done.1
  49.9 0.0 copy-done.2
  49.9 0.0 copy-done.4
  49.9 0.0 copy-done.5
  49.9 39.1 %solve.1 = (f32[25,64]{1,0:T(8,128)S(1)}, f32[25,64]{1,0:T(8,128)S(1)}) custom-call(s32[1,2]{1,0:T(1,128)S(1)} %copy-done.4, s32[1,2]{1,0:T(1,128)S(1)} %copy-done.5, s32[8,128]{1,0:T(8,128)S(1)} %concatenate.11.ints_ref, bf16[32,256]{1,0:T(8,128)(2,1)S(1)} %copy-done.2, bf16[256,32]{1,0:T(8,128)(2,1)S(1)} %copy-done.1, ...), custom_call_target="tpu_custom_call" | custom-call | tf_op jit(solution)/shard_map/solve/pallas_call | solution.py:464
  89.0 0.6 copy.15
  89.6 0.6 copy.16
  (7 shorter events, 0.0 us)
Async XLA Ops:
  4.7 2.5 %copy-start = (f32[12,275,275]{2,1,0:T(8,128)S(1)}, f32[12,275,275]{2,1,0:T(8,128)}, u32[]{:S(2)}) copy-start(f32[12,275,275]{2,1,0:T(8,128)} %basis_ref.1) | copy-start | bytes 10890004
  7.2 0.7 copy-start.3
  7.9 42.0 %copy-start.1 = (bf16[256,32]{1,0:T(8,128)(2,1)S(1)}, bf16[256,32]{1,0:T(8,128)(2,1)}, u32[]{:S(2)}) copy-start(bf16[256,32]{1,0:T(8,128)(2,1)} %constant.14.clone.permt_ref) | copy-start | bytes 49156
  7.9 42.0 %copy-start.2 = (bf16[32,256]{1,0:T(8,128)(2,1)S(1)}, bf16[32,256]{1,0:T(8,128)(2,1)}, u32[]{:S(2)}) copy-start(bf16[32,256]{1,0:T(8,128)(2,1)} %constant.13.clone.perm_ref) | copy-start | bytes 49156
  7.9 42.0 %copy-start.4 = (s32[1,2]{1,0:T(1,128)S(1)}, s32[1,2]{1,0:T(1,128)}, u32[]{:S(2)}) copy-start(s32[1,2]{1,0:T(1,128)} %upper_ref.1) | copy-start | bytes 28
  7.9 42.0 %copy-start.5 = (s32[1,2]{1,0:T(1,128)S(1)}, s32[1,2]{1,0:T(1,128)}, u32[]{:S(2)}) copy-start(s32[1,2]{1,0:T(1,128)} %lower_ref.1) | copy-start | bytes 28

commit v2 on v1

--- a/solution.py
+++ b/solution.py
@@ -20,6 +20,7 @@
 LANES = 128
 ROWS = 160
 NB = 32
+WAYS = 4
 BF = jnp.bfloat16
 F32 = jnp.float32
 
@@ -100,7 +101,7 @@
     return tiles
 
 
-def condense_kernel(elems, terms, coef_ref, basis_ref, load_ref, shi_ref, slo_ref, diag_ref, lrow_ref, x_ref, d_ref):
+def condense_kernel(elems, terms, coef_ref, basis_ref, load_ref, shi_ref, slo_ref, diag_ref, lrow_ref, x_refs, d_ref, r_refs):
     lane8 = iota((8, LANES), 1)
     sub8 = iota((8, LANES), 0)
     tail = LOCAL_DOFS - 256
@@ -123,6 +124,10 @@
                 )
             emit(e, t0, t1, t2)
 
+    def put(e, start, *tiles):
+        for i, tile in enumerate(tiles):
+            x_refs[e % WAYS][e // WAYS, pl.ds(start, 8), LANES * i : LANES * i + LANES] = tile
+
     def put_inner(e, start, t0, t1, t2, edge):
         inner = lane8 < CELL_DOFS
         moved = jnp.where(inner, t2, t0)
@@ -132,15 +137,11 @@
             kept = jnp.where(good, kept, jnp.where(sub8 + 120 == lane8, 1.0, 0.0))
             t1 = jnp.where(good, t1, 0.0)
             moved = jnp.where(good, moved, 0.0)
-        x_ref[e, pl.ds(start, 8), 0:128] = kept
-        x_ref[e, pl.ds(start, 8), 128:256] = t1
-        x_ref[e, pl.ds(start, 8), 256:384] = moved
+        put(e, start, kept, t1, moved)
 
     def put_outer(e, start, t0, t1, t2):
         inner = lane8 < CELL_DOFS
-        x_ref[e, pl.ds(start, 8), 0:128] = jnp.where(inner, t0, 0.0)
-        x_ref[e, pl.ds(start, 8), 128:256] = t1
-        x_ref[e, pl.ds(start, 8), 256:384] = jnp.where(inner, t2, t0)
+        put(e, start, jnp.where(inner, t0, 0.0), t1, jnp.where(inner, t2, t0))
 
     @pl.loop(0, 15)
     def _(t):
@@ -173,7 +174,7 @@
         for g in range(groups):
             whole = jnp.zeros((NB, LANES), F32)
             for q in range(4):
-                part = x_ref[g * 4 + q, rows, 0:128]
+                part = x_refs[q][g, rows, 0:128]
                 shift = (NB * (q - b)) % LANES
                 if shift:
                     part = pltpu.roll(part, shift, 1)
@@ -186,29 +187,38 @@
                 d_ref[g * 4 + q] = pack_lanes(whole, NB * q)
         lo = 0 if b < 3 else LANES
 
-        @pl.loop(0, elems)
-        def _(e):
-            scaled = jnp.dot(d_ref[e], pack_rows(x_ref[e, rows, lo:384]), preferred_element_type=F32)
-            lhs = pack_lanes(x_ref[e, NB * (b + 1) : 288, 0:128], NB * b)
-            update = jnp.dot(lhs, pack_rows(scaled), preferred_element_type=F32)
-            x_ref[e, NB * (b + 1) : 288, lo:384] = x_ref[e, NB * (b + 1) : 288, lo:384] - update
+        below = slice(NB * (b + 1), 288)
+
+        @pl.loop(0, groups)
+        def _(g):
+            for q in range(WAYS):
+                scaled = jnp.dot(
+                    d_ref[g * WAYS + q], pack_rows(x_refs[q][g, rows, lo:384]), preferred_element_type=F32
+                )
+                r_refs[q][:, lo:384] = pack_rows(scaled)
+            for q in range(WAYS):
+                lhs = pack_lanes(x_refs[q][g, below, 0:128], NB * b)
+                update = jnp.dot(lhs, r_refs[q][:, lo:384], preferred_element_type=F32)
+                x_refs[q][g, below, lo:384] = x_refs[q][g, below, lo:384] - update
 
     diag_ref[...] = jnp.zeros_like(diag_ref)
     lane_w = iota((ROWS, 256), 1)
     on_diag = (iota((ROWS, 256), 0) + 248) % 256 == lane_w
     lane_t = iota((ROWS, LANES), 1)
 
-    @pl.loop(0, elems)
-    def _(e):
-        s = x_ref[e, 128:288, 128:384]
-        high = s.astype(BF)
-        start = pl.multiple_of(e * ROWS, 32)
-        shi_ref[pl.ds(start, ROWS), :] = high
-        slo_ref[pl.ds(start, ROWS), :] = (s - high.astype(F32)).astype(BF)
-        only = jnp.where(on_diag, s, 0.0)
-        column = jnp.sum(only[:, 0:128] + only[:, 128:256], axis=1, keepdims=True)
-        diag_ref[...] = jnp.where(lane_t == e, column, diag_ref[...])
-        lrow_ref[pl.ds(e, 1), :] = s[0:1, :]
+    @pl.loop(0, groups)
+    def _(g):
+        for q in range(WAYS):
+            e = g * WAYS + q
+            s = x_refs[q][g, 128:288, 128:384]
+            high = s.astype(BF)
+            start = pl.multiple_of(e * ROWS, 32)
+            shi_ref[pl.ds(start, ROWS), :] = high
+            slo_ref[pl.ds(start, ROWS), :] = (s - high.astype(F32)).astype(BF)
+            only = jnp.where(on_diag, s, 0.0)
+            column = jnp.sum(only[:, 0:128] + only[:, 128:256], axis=1, keepdims=True)
+            diag_ref[...] = jnp.where(lane_t == e, column, diag_ref[...])
+            lrow_ref[pl.ds(e, 1), :] = s[0:1, :]
 
 
 def split3(x):
@@ -438,7 +448,11 @@
         ),
         in_specs=[smem, vmem, vmem],
         out_specs=(vmem, vmem, vmem, vmem),
-        scratch_shapes=[pltpu.VMEM((elems, 288, 384), F32), pltpu.VMEM((elems, NB, LANES), BF)],
+        scratch_shapes=[
+            [pltpu.VMEM((elems // WAYS, 288, 384), F32)] * WAYS,
+            pltpu.VMEM((elems, NB, LANES), BF),
+            [pltpu.VMEM((LANES, 384), BF)] * WAYS,
+        ],
         compiler_params=pltpu.CompilerParams(vmem_limit_bytes=40 * 1024 * 1024),
         name="condense",
     )(coeffs, basis_mats, loads)

time: 90.6 us -> 76.6 us (0.85)
  Pallas kernels: 81.1 us -> 67 us
    pallas_call x1, Pallas kernels: 42 us -> 28 us  [on_device(): pl.pallas_call(functools.partial(condense_kernel, elems, terms), out_shap...]
where the time goes in v2:
time: 76.6 us; the launch traced here: 76.2 us
  Pallas kernels  67 us (87%)
  local copies, waits for them, and re-layouts  7.72 us (10%)
    pallas_call x1, Pallas kernels, on_device(): pl.pallas_call(functools.partial(cg_kernel, ('gx', 'gy'), sizes, elems),...  39.1 us
    pallas_call x1, Pallas kernels, on_device(): pl.pallas_call(functools.partial(condense_kernel, elems, terms), out_shap...  28 us
    unnamed x14, local copies, waits for them, and re-layouts  4.39 us

profile of v2, /device:TPU:0, one launch (start us, length us, event | category | flops | bytes accessed | tf_op | source)
XLA Modules:
  0.0 76.2 jit_solution(2821492503441781425)
XLA Ops:
  0.6 0.8 %reshape.18 = s32[1,96]{1,0:T(1,128)S(1)} reshape(s32[6,16]{1,0:T(8,128)} %bitcast.2) | data formatting | bytes 768 | tf_op jit(solution)/shard_map/reshape | solution.py:461
  1.4 0.8 %reshape.19 = s32[1,96]{1,0:T(1,128)S(1)} reshape(s32[6,16]{1,0:T(8,128)} %bitcast.3) | data formatting | bytes 768 | tf_op jit(solution)/shard_map/reshape | solution.py:461
  2.2 0.8 reshape.20
  2.9 0.7 broadcast_add_fusion
  3.6 0.1 add.13
  3.7 0.1 pad_add_fusion.1
  3.8 0.1 broadcast_in_dim_tile.7
  3.9 0.1 broadcast_in_dim_tile.6
  4.0 0.7 pad.13.load_ref
  4.7 0.0 copy-start
  4.7 2.5 %copy-done = f32[12,275,275]{2,1,0:T(8,128)S(1)} copy-done((f32[12,275,275]{2,1,0:T(8,128)S(1)}, f32[12,275,275]{2,1,0:T(8,128)}, u32[]{:S(2)}) %copy-start) | copy-done | bytes 3630024
  7.2 0.0 copy-start.3
  7.2 0.7 copy-done.3
  7.9 0.0 copy-start.1
  7.9 0.0 copy-start.2
  7.9 0.0 copy-start.4
  7.9 28.0 %condense.1 = (bf16[2560,256]{1,0:T(8,128)(2,1)S(1)}, bf16[2560,256]{1,0:T(8,128)(2,1)S(1)}, f32[160,128]{1,0:T(8,128)S(1)}, f32[16,256]{1,0:T(8,128)S(1)}) custom-call(f32[16,12]{1,0:T(8,128)S(1)} %copy-done.3, f32[12,275,275]{2,1,0:T(8,128)S(1)} %copy-done, f32[16,384]{1,0:T(8,128)S(1)} %pad.13.load_ref), custom_call_target="tpu_custom_call" | custom-call | tf_op jit(solution)/shard_map/condense/pallas_call | solution.py:441
  35.9 0.0 copy-done.1
  35.9 0.0 copy-done.2
  35.9 0.0 copy-done.4
  35.9 0.0 copy-done.5
  35.9 39.1 %solve.1 = (f32[25,64]{1,0:T(8,128)S(1)}, f32[25,64]{1,0:T(8,128)S(1)}) custom-call(s32[1,2]{1,0:T(1,128)S(1)} %copy-done.4, s32[1,2]{1,0:T(1,128)S(1)} %copy-done.5, s32[8,128]{1,0:T(8,128)S(1)} %concatenate.11.ints_ref, bf16[32,256]{1,0:T(8,128)(2,1)S(1)} %copy-done.2, bf16[256,32]{1,0:T(8,128)(2,1)S(1)} %copy-done.1, ...), custom_call_target="tpu_custom_call" | custom-call | tf_op jit(solution)/shard_map/solve/pallas_call | solution.py:478
  75.0 0.6 copy.15
  75.6 0.6 copy.16
  (7 shorter events, 0.0 us)
Async XLA Ops:
  4.7 2.5 %copy-start = (f32[12,275,275]{2,1,0:T(8,128)S(1)}, f32[12,275,275]{2,1,0:T(8,128)}, u32[]{:S(2)}) copy-start(f32[12,275,275]{2,1,0:T(8,128)} %basis_ref.1) | copy-start | bytes 10890004
  7.2 0.7 copy-start.3
  7.9 28.0 %copy-start.1 = (bf16[256,32]{1,0:T(8,128)(2,1)S(1)}, bf16[256,32]{1,0:T(8,128)(2,1)}, u32[]{:S(2)}) copy-start(bf16[256,32]{1,0:T(8,128)(2,1)} %constant.14.clone.permt_ref) | copy-start | bytes 49156
  7.9 28.0 %copy-start.2 = (bf16[32,256]{1,0:T(8,128)(2,1)S(1)}, bf16[32,256]{1,0:T(8,128)(2,1)}, u32[]{:S(2)}) copy-start(bf16[32,256]{1,0:T(8,128)(2,1)} %constant.13.clone.perm_ref) | copy-start | bytes 49156
  7.9 28.0 %copy-start.4 = (s32[1,2]{1,0:T(1,128)S(1)}, s32[1,2]{1,0:T(1,128)}, u32[]{:S(2)}) copy-start(s32[1,2]{1,0:T(1,128)} %upper_ref.1) | copy-start | bytes 28
  7.9 28.0 %copy-start.5 = (s32[1,2]{1,0:T(1,128)S(1)}, s32[1,2]{1,0:T(1,128)}, u32[]{:S(2)}) copy-start(s32[1,2]{1,0:T(1,128)} %lower_ref.1) | copy-start | bytes 28

commit v3 on v2

--- a/solution.py
+++ b/solution.py
@@ -20,6 +20,7 @@
 LANES = 128
 ROWS = 160
 NB = 32
+CUTS = (0, 64, 128, 200, 275)
 WAYS = 4
 BF = jnp.bfloat16
 F32 = jnp.float32
@@ -75,33 +76,67 @@
     return jnp.concatenate([high, high, low, jnp.zeros_like(high)], axis=0)
 
 
+def inverse2(m):
+    (a, b), (c, d) = m
+    scale = 1.0 / (a * d - b * c)
+    return (d * scale, -b * scale), (-c * scale, a * scale)
+
+
+def times2(m, n):
+    return tuple(tuple(m[i][0] * n[0][j] + m[i][1] * n[1][j] for j in range(len(n[0]))) for i in range(2))
+
+
+def minus2(m, n):
+    return tuple(tuple(a - b for a, b in zip(x, y)) for x, y in zip(m, n))
+
+
 def invert_blocks(tiles):
     lane = iota((8, LANES), 1)
     sub = iota((8, LANES), 0)
     inside = lane % NB
     first = lane - inside
-    for k in range(NB):
+    for k in range(0, NB, 4):
         tk, sk = k // 8, k % 8
-        pick = first + k
-        here = inside == k
+        here = inside // 4 == k // 4
         for g in range(len(tiles)):
             group = tiles[g]
-            row = jnp.broadcast_to(group[tk][sk : sk + 1, :], (8, LANES))
-            pivot = jnp.take_along_axis(row, pick, axis=1)
-            inverse = 1.0 / pivot
-            new_row = jnp.where(here, inverse, row * inverse)
+            columns = [
+                [jnp.take_along_axis(group[t], first + (k + m), axis=1) for t in range(4)] for m in range(4)
+            ]
+
+            def spread(value, i):
+                return jnp.broadcast_to(value[sk + i : sk + i + 1, :], (8, LANES))
+
+            def block(i, j):
+                return tuple(tuple(spread(columns[n][tk], m) for n in (j, j + 1)) for m in (i, i + 1))
+
+            rows = [
+                (jnp.where(here, jnp.where(inside == k + m, 1.0, 0.0), spread(group[tk], m)),) for m in range(4)
+            ]
+            a_inv = inverse2(block(0, 0))
+            c = block(2, 0)
+            t_block = times2(a_inv, block(0, 2))
+            s_inv = inverse2(minus2(block(2, 2), times2(c, t_block)))
+            upper = times2(a_inv, (rows[0], rows[1]))
+            lower = times2(s_inv, minus2((rows[2], rows[3]), times2(c, upper)))
+            upper = minus2(upper, times2(t_block, lower))
+            fresh_rows = [upper[0][0], upper[1][0], lower[0][0], lower[1][0]]
             fresh = []
             for t in range(4):
-                column = jnp.take_along_axis(group[t], pick, axis=1)
-                value = jnp.where(here, 0.0, group[t]) - column * new_row
+                value = jnp.where(here, 0.0, group[t])
+                value = value - (
+                    (columns[0][t] * fresh_rows[0] + columns[1][t] * fresh_rows[1])
+                    + (columns[2][t] * fresh_rows[2] + columns[3][t] * fresh_rows[3])
+                )
                 if t == tk:
-                    value = jnp.where(sub == sk, new_row, value)
+                    for m in range(4):
+                        value = jnp.where(sub == sk + m, fresh_rows[m], value)
                 fresh.append(value)
             tiles[g] = fresh
     return tiles
 
 
-def condense_kernel(elems, terms, coef_ref, basis_ref, load_ref, shi_ref, slo_ref, diag_ref, lrow_ref, x_refs, d_ref, r_refs):
+def condense(elems, terms, coef_ref, basis_ref, arrived, load_ref, shi_ref, slo_ref, diag_ref, lrow_ref, x_refs, d_ref, r_refs):
     lane8 = iota((8, LANES), 1)
     sub8 = iota((8, LANES), 0)
     tail = LOCAL_DOFS - 256
@@ -143,27 +178,37 @@
         inner = lane8 < CELL_DOFS
         put(e, start, jnp.where(inner, t0, 0.0), t1, jnp.where(inner, t2, t0))
 
-    @pl.loop(0, 15)
-    def _(t):
+    def inner_rows(t):
         start = pl.multiple_of(t * 8, 8)
         combine(pl.ds(start, 8), 8, lambda e, a, b, c: put_inner(e, start, a, b, c, False))
+
+    def outer_rows(t):
+        start = pl.multiple_of(t * 8, 8)
+        combine(pl.ds(start, 8), 8, lambda e, a, b, c: put_outer(e, start + 8, a, b, c))
+
+    arrived(0)
+    pl.loop(0, CUTS[1] // 8)(inner_rows)
+    arrived(1)
+    pl.loop(CUTS[1] // 8, 15)(inner_rows)
 
     def edge_rows(e, t0, t1, t2):
         put_inner(e, 120, t0, t1, t2, True)
         first = sub8 == 0
 
         def with_load(tile, lo):
-            return jnp.where(first, jnp.broadcast_to(load_ref[e : e + 1, lo : lo + 128], (8, LANES)), tile)
+            row = load_ref[e : e + 1, lo : min(lo + LANES, LOCAL_DOFS)]
+            if row.shape[1] < LANES:
+                row = jnp.concatenate([row, jnp.zeros((1, LANES - row.shape[1]), F32)], axis=1)
+            return jnp.where(first, jnp.broadcast_to(row, (8, LANES)), tile)
 
         put_outer(e, 128, with_load(t0, 0), with_load(t1, 128), with_load(t2, 256))
 
     combine(pl.ds(120, 8), 8, edge_rows)
 
-    @pl.loop(16, 34)
-    def _(t):
-        start = pl.multiple_of(t * 8, 8)
-        combine(pl.ds(start, 8), 8, lambda e, a, b, c: put_outer(e, start + 8, a, b, c))
-
+    arrived(2)
+    pl.loop(16, CUTS[3] // 8)(outer_rows)
+    arrived(3)
+    pl.loop(CUTS[3] // 8, 34)(outer_rows)
     combine(pl.ds(272, 3), 3, lambda e, a, b, c: put_outer(e, 280, a, b, c))
 
     groups = elems // 4
@@ -229,12 +274,20 @@
     return a, b, c
 
 
-def cg_kernel(
-    mesh_names, sizes, elems, upper_ref, lower_ref, ints_ref, perm_ref, permt_ref, shi_ref, slo_ref, diag_ref, lrow_ref,
-    trace_ref, resid_ref, buf_refs, send_ref, send_sem, recv_sem,
+def kernel(
+    mesh_names, sizes, elems, terms, coef_ref, upper_ref, lower_ref, owned_ref, remote_ref, basis_hbm, load_ref, face_ref,
+    code_ref, perm_ref, permt_ref, trace_ref, resid_ref, basis_ref, shi_ref, slo_ref, diag_ref, lrow_ref, x_refs, d_ref,
+    r_refs, buf_refs, send_ref, basis_sem, send_sem, recv_sem,
 ):
     devices = sizes[0] * sizes[1]
     me = lax.axis_index(mesh_names[0]) * sizes[1] + lax.axis_index(mesh_names[1])
+
+    def chunk(i):
+        rows = slice(CUTS[i], CUTS[i + 1])
+        return pltpu.make_async_copy(basis_hbm.at[:, rows, :], basis_ref.at[:, rows, :], basis_sem.at[i])
+
+    for i in range(4):
+        chunk(i).start()
 
     def coords(d):
         return (d // sizes[1], lax.rem(d, sizes[1]))
@@ -249,19 +302,46 @@
 
     lax.fori_loop(1, devices, greet, 0)
 
+    condense(
+        elems, terms, coef_ref, basis_ref, lambda i: chunk(i).wait(), load_ref, shi_ref, slo_ref, diag_ref, lrow_ref,
+        x_refs, d_ref, r_refs,
+    )
+
     square = (LANES, LANES)
     sub = iota(square, 0)
-    inc_t = jnp.where(sub == ints_ref[0:1, :], 1.0, 0.0)
+    lane1 = iota((1, LANES), 1)
+
+    def in_lanes(ref, fill):
+        wide = jnp.concatenate([ref[...].astype(F32), jnp.zeros((elems, LANES - 6), F32)], axis=1)
+        turned = jnp.concatenate([wide, jnp.zeros((LANES - elems, LANES), F32)], axis=0).T
+        out = jnp.full((1, LANES), fill, F32)
+        for j in range(6):
+            row = turned[j : j + 1]
+            if j:
+                row = pltpu.roll(row, 16 * j, 1)
+            out = jnp.where(lane1 // 16 == j, row, out)
+        return out
+
+    def listed(first, second):
+        out = jnp.zeros((1, LANES), jnp.int32)
+        for at, (ref, base) in enumerate((first, second)):
+            for i in range(2):
+                for k in range(SHARED):
+                    out = jnp.where(lane1 % 16 == 8 * at + SHARED * i + k, base + ref[0, i, k], out)
+        return out
+
+    own, far = (owned_ref, 0), (remote_ref, FACE_DEV)
+    inc_t = jnp.where(sub.astype(F32) == in_lanes(face_ref, -1.0), 1.0, 0.0)
     inc = inc_t.T
-    sel = jnp.where(sub == ints_ref[2:3, :], 1.0, 0.0).astype(BF)
-    place = jnp.where(sub == ints_ref[3:4, :], 1.0, 0.0).T.astype(BF)
+    sel = jnp.where(sub == listed(own, far), 1.0, 0.0).astype(BF)
+    place = jnp.where(sub == listed(far, own), 1.0, 0.0).T.astype(BF)
     inc_t = inc_t.astype(BF)
     inc = inc.astype(BF)
     inc_sel = jnp.dot(inc, sel, preferred_element_type=F32).astype(BF)
     out_mat = jnp.concatenate([inc, inc_sel], axis=1)
     perm = perm_ref[...]
     perm_t = permt_ref[...]
-    code = ints_ref[1:2, :]
+    code = in_lanes(code_ref, 0.0)
     lane32 = iota((32, LANES), 1)
     sub32 = iota((32, LANES), 0)
     in_group = lane32 // 16 == sub32 // 4
@@ -437,64 +517,38 @@
     elems, terms = coeffs.shape
     vmem = pl.BlockSpec(memory_space=pltpu.VMEM)
     smem = pl.BlockSpec(memory_space=pltpu.SMEM)
-    loads = jnp.pad(element_loads, ((0, 0), (0, 384 - LOCAL_DOFS)))
-    shi, slo, diag, lrow = pl.pallas_call(
-        functools.partial(condense_kernel, elems, terms),
-        out_shape=(
-            jax.ShapeDtypeStruct((elems * ROWS, 256), BF),
-            jax.ShapeDtypeStruct((elems * ROWS, 256), BF),
-            jax.ShapeDtypeStruct((ROWS, LANES), F32),
-            jax.ShapeDtypeStruct((elems, 256), F32),
-        ),
-        in_specs=[smem, vmem, vmem],
-        out_specs=(vmem, vmem, vmem, vmem),
-        scratch_shapes=[
-            [pltpu.VMEM((elems // WAYS, 288, 384), F32)] * WAYS,
-            pltpu.VMEM((elems, NB, LANES), BF),
-            [pltpu.VMEM((LANES, 384), BF)] * WAYS,
-        ],
-        compiler_params=pltpu.CompilerParams(vmem_limit_bytes=40 * 1024 * 1024),
-        name="condense",
-    )(coeffs, basis_mats, loads)
-
-    def lane_row(values, fill):
-        flat = values.reshape(1, -1)
-        return jnp.pad(flat, ((0, 0), (0, LANES - flat.shape[1])), constant_values=fill)
-
-    own = shared_owned.reshape(-1)
-    far = FACE_DEV + shared_remote.reshape(-1)
-    ints = jnp.concatenate(
-        [
-            lane_row(elem_faces.T, -1),
-            lane_row(orient_codes.T, 0),
-            jnp.tile(jnp.concatenate([own, far]), 8)[None],
-            jnp.tile(jnp.concatenate([far, own]), 8)[None],
-            jnp.zeros((4, LANES), jnp.int32),
-        ],
-        axis=0,
-    )
     stack = permute_stack()
     devices = sizes[0] * sizes[1]
     return pl.pallas_call(
-        functools.partial(cg_kernel, ("gx", "gy"), sizes, elems),
+        functools.partial(kernel, ("gx", "gy"), sizes, elems, terms),
         out_shape=(
             jax.ShapeDtypeStruct((FACE_DOFS, FACE_DEV), F32),
             jax.ShapeDtypeStruct((FACE_DOFS, FACE_DEV), F32),
         ),
-        in_specs=[smem, smem] + [vmem] * 7,
+        in_specs=[smem] * 5 + [pl.BlockSpec(memory_space=pltpu.HBM)] + [vmem] * 5,
         out_specs=(vmem, vmem),
         scratch_shapes=[
+            pltpu.VMEM((terms, LOCAL_DOFS, LOCAL_DOFS), F32),
+            pltpu.VMEM((elems * ROWS, 256), BF),
+            pltpu.VMEM((elems * ROWS, 256), BF),
+            pltpu.VMEM((ROWS, LANES), F32),
+            pltpu.VMEM((elems, 256), F32),
+            [pltpu.VMEM((elems // WAYS, 288, 384), F32)] * WAYS,
+            pltpu.VMEM((elems, NB, LANES), BF),
+            [pltpu.VMEM((LANES, 384), BF)] * WAYS,
             [pltpu.VMEM((devices, 8 if i == 0 else 4, LANES), F32) for i in range(ITERS + 1)],
             pltpu.VMEM((ITERS + 1, 8, LANES), F32),
+            pltpu.SemaphoreType.DMA((4,)),
             pltpu.SemaphoreType.DMA((ITERS + 1,)),
             pltpu.SemaphoreType.DMA((ITERS + 1,)),
         ],
         compiler_params=pltpu.CompilerParams(
-            collective_id=0, has_side_effects=True, vmem_limit_bytes=48 * 1024 * 1024
+            collective_id=0, has_side_effects=True, vmem_limit_bytes=56 * 1024 * 1024
         ),
-        name="solve",
+        name="hdg",
     )(
-        upper_peers, lower_peers, ints, jnp.asarray(stack, BF), jnp.asarray(stack.T, BF), shi, slo, diag, lrow
+        coeffs, upper_peers, lower_peers, shared_owned, shared_remote, basis_mats, element_loads, elem_faces, orient_codes,
+        jnp.asarray(stack, BF), jnp.asarray(stack.T, BF),
     )
 
 

time: 76.6 us -> 67.2 us (0.88)
  Pallas kernels: 67 us -> 60.8 us
  local copies, waits for them, and re-layouts: 7.72 us -> 5.37 us
    pallas_call x2 -> x1, Pallas kernels: 67 us -> 60.8 us  [on_device(): pl.pallas_call(functools.partial(kernel, ('gx', 'gy'), sizes, elems, term...]
    reshape x3 -> x0, local copies, waits for them, and re-layouts: 2.29 us -> none  [the longest x2 1.53 us: lane_row(): flat = values.reshape(1, -1)]
    unnamed x14 -> x4, local copies, waits for them, and re-layouts: 4.39 us -> 5.37 us
where the time goes in v3:
time: 67.2 us; the launch traced here: 66.8 us
  Pallas kernels  60.8 us (90%)
  local copies, waits for them, and re-layouts  5.37 us (8%)
    pallas_call x1, Pallas kernels, on_device(): pl.pallas_call(functools.partial(kernel, ('gx', 'gy'), sizes, elems, term...  60.8 us
    unnamed x4, local copies, waits for them, and re-layouts  5.37 us

profile of v3, /device:TPU:0, one launch (start us, length us, event | category | flops | bytes accessed | tf_op | source)
XLA Modules:
  0.0 66.8 jit_solution(8603439212648395803)
XLA Ops:
  0.6 1.4 %copy.13.face_ref = s32[16,6]{1,0:T(8,128)} copy(s32[16,6]{0,1:T(8,128)} %param.14) | data formatting | bytes 768 | tf_op args[3]
  2.0 1.4 %copy.14.code_ref = s32[16,6]{1,0:T(8,128)} copy(s32[16,6]{0,1:T(8,128)} %param.15) | data formatting | bytes 768 | tf_op args[4]
  3.4 60.8 %hdg.1 = (f32[25,64]{1,0:T(8,128)}, f32[25,64]{1,0:T(8,128)}) custom-call(f32[16,12]{1,0:T(8,128)} %coef_ref.1, s32[1,2]{1,0:T(1,128)} %upper_ref.1, s32[1,2]{1,0:T(1,128)} %lower_ref.1, s32[1,2,4]{2,1,0:T(2,128)} %owned_ref.1, s32[1,2,4]{2,1,0:T(2,128)} %remote_ref.1, f32[12,275,275]{2,1,0:T(8,128)} %basis_hbm.1, f32[16,275]{1,0:T(8,128)} %load_ref.1, ...), custom_call_target="tpu_custom_call" | custom-call | tf_op jit(solution)/shard_map/hdg/pallas_call | solution.py:522
  64.2 1.3 %copy.17 = f32[25,64]{1,0:T(8,128)} copy(f32[25,64]{1,0:T(8,128)} %get-tuple-element.4) | data formatting | bytes 12800
  65.5 1.3 %copy.18 = f32[25,64]{1,0:T(8,128)} copy(f32[25,64]{1,0:T(8,128)} %get-tuple-element.5) | data formatting | bytes 12800

commit v4 on v3

--- a/solution.py
+++ b/solution.py
@@ -276,7 +276,7 @@
 
 def kernel(
     mesh_names, sizes, elems, terms, coef_ref, upper_ref, lower_ref, owned_ref, remote_ref, basis_hbm, load_ref, face_ref,
-    code_ref, perm_ref, permt_ref, trace_ref, resid_ref, basis_ref, shi_ref, slo_ref, diag_ref, lrow_ref, x_refs, d_ref,
+    code_ref, perm_ref, permt_ref, out_ref, basis_ref, shi_ref, slo_ref, diag_ref, lrow_ref, x_refs, d_ref,
     r_refs, buf_refs, send_ref, basis_sem, send_sem, recv_sem,
 ):
     devices = sizes[0] * sizes[1]
@@ -312,8 +312,7 @@
     lane1 = iota((1, LANES), 1)
 
     def in_lanes(ref, fill):
-        wide = jnp.concatenate([ref[...].astype(F32), jnp.zeros((elems, LANES - 6), F32)], axis=1)
-        turned = jnp.concatenate([wide, jnp.zeros((LANES - elems, LANES), F32)], axis=0).T
+        turned = jnp.concatenate([ref[...].astype(F32), jnp.zeros((6, LANES - elems), F32)], axis=1)
         out = jnp.full((1, LANES), fill, F32)
         for j in range(6):
             row = turned[j : j + 1]
@@ -417,18 +416,30 @@
             send_ref[slot, 4 * i : 4 * i + 4] = part
             buf_ref[me, 4 * i : 4 * i + 4] = part
 
-        def send(k, carry):
+        def send(first, second):
             pltpu.make_async_remote_copy(
                 src_ref=own_rows,
                 dst_ref=buf_ref.at[me],
                 send_sem=send_sem.at[slot],
                 recv_sem=recv_sem.at[slot],
-                device_id=coords(lax.rem(me + k, devices)),
+                device_id=(
+                    lax.rem(lax.axis_index(mesh_names[0]) + first, sizes[0]),
+                    lax.rem(lax.axis_index(mesh_names[1]) + second, sizes[1]),
+                ),
                 device_id_type=pl.DeviceIdType.MESH,
             ).start()
+
+        def send_at(k, carry):
+            send(k // sizes[1], lax.rem(k, sizes[1]))
             return carry
 
-        lax.fori_loop(1, devices, send, 0)
+        if devices > 64:
+            lax.fori_loop(1, devices, send_at, 0)
+        else:
+            for second in sorted(range(sizes[1]), key=lambda k: -min(k, sizes[1] - k)):
+                for first in reversed(range(sizes[0])):
+                    if first or second:
+                        send(first, second)
         every = buf_ref.at[pl.ds(0, devices - 1)]
         pltpu.make_async_copy(every, every, recv_sem.at[slot]).wait()
         pltpu.make_async_copy(every, every, send_sem.at[slot]).wait()
@@ -489,10 +500,7 @@
         slot = iteration + 1
         got = exchange(slot, [message])[0]
 
-        def add(d, carry):
-            return carry + buf_refs[slot][d]
-
-        sums = lax.fori_loop(0, devices, add, jnp.zeros((4, LANES), F32))
+        sums = jnp.sum(buf_refs[slot][...], axis=0)
         rz_next = jnp.sum(jnp.where(spare & (slot4 == 0), sums, 0.0), keepdims=True)
         curve = jnp.sum(jnp.where(spare & (slot4 == 1), sums, 0.0), keepdims=True)
         mapped = jnp.where(live, part + got, 0.0)
@@ -507,8 +515,8 @@
         rz_now = rz_next
         trace = trace + step * direction
         residual = residual - step * image
-    trace_ref[...] = trace[0:FACE_DOFS, 0:FACE_DEV]
-    resid_ref[...] = residual[0:FACE_DOFS, 0:FACE_DEV]
+    out_ref[0] = trace
+    out_ref[1] = residual
 
 
 def on_device(
@@ -519,14 +527,11 @@
     smem = pl.BlockSpec(memory_space=pltpu.SMEM)
     stack = permute_stack()
     devices = sizes[0] * sizes[1]
-    return pl.pallas_call(
+    result = pl.pallas_call(
         functools.partial(kernel, ("gx", "gy"), sizes, elems, terms),
-        out_shape=(
-            jax.ShapeDtypeStruct((FACE_DOFS, FACE_DEV), F32),
-            jax.ShapeDtypeStruct((FACE_DOFS, FACE_DEV), F32),
-        ),
+        out_shape=jax.ShapeDtypeStruct((2, 32, LANES), F32),
         in_specs=[smem] * 5 + [pl.BlockSpec(memory_space=pltpu.HBM)] + [vmem] * 5,
-        out_specs=(vmem, vmem),
+        out_specs=vmem,
         scratch_shapes=[
             pltpu.VMEM((terms, LOCAL_DOFS, LOCAL_DOFS), F32),
             pltpu.VMEM((elems * ROWS, 256), BF),
@@ -547,9 +552,10 @@
         ),
         name="hdg",
     )(
-        coeffs, upper_peers, lower_peers, shared_owned, shared_remote, basis_mats, element_loads, elem_faces, orient_codes,
+        coeffs, upper_peers, lower_peers, shared_owned, shared_remote, basis_mats, element_loads, elem_faces.T, orient_codes.T,
         jnp.asarray(stack, BF), jnp.asarray(stack.T, BF),
     )
+    return result[0, :FACE_DOFS, :FACE_DEV], result[1, :FACE_DOFS, :FACE_DEV]
 
 
 def solution(mesh):

time: 67.2 us -> 63.9 us (0.951)
  local copies, waits for them, and re-layouts: 5.37 us -> 1.35 us
  Pallas kernels: 60.8 us -> 61.7 us
    unnamed x4 -> x0, local copies, waits for them, and re-layouts: 5.37 us -> none
    squeeze x0 -> x1, local copies, waits for them, and re-layouts: none -> 1.35 us  [on_device(): return (result[0, :FACE_DOFS, :FACE_DEV], result[1, :FACE_DOFS, :FACE_DEV])]
    pallas_call x1, Pallas kernels: 60.8 us -> 61.7 us  [on_device(): pl.pallas_call(functools.partial(kernel, ('gx', 'gy'), sizes, elems, term...]
where the time goes in v4:
time: 63.9 us; the launch traced here: 63.7 us
  Pallas kernels  61.7 us (97%)
  local copies, waits for them, and re-layouts  1.35 us (2%)
  between operations  0.64 us (1%)
    pallas_call x1, Pallas kernels, on_device(): pl.pallas_call(functools.partial(kernel, ('gx', 'gy'), sizes, elems, term...  61.7 us
    squeeze x1, local copies, waits for them, and re-layouts, on_device(): return (result[0, :FACE_DOFS, :FACE_DEV], result[1, :FACE_DOFS, :FACE_DEV])  1.35 us

profile of v4, /device:TPU:0, one launch (start us, length us, event | category | flops | bytes accessed | tf_op | source)
XLA Modules:
  0.0 63.7 jit_solution(8128284485401296310)
XLA Ops:
  0.6 61.7 %hdg.1 = f32[2,32,128]{2,1,0:T(8,128)} custom-call(f32[16,12]{1,0:T(8,128)} %coef_ref.1, s32[1,2]{1,0:T(1,128)} %upper_ref.1, s32[1,2]{1,0:T(1,128)} %lower_ref.1, s32[1,2,4]{2,1,0:T(2,128)} %owned_ref.1, s32[1,2,4]{2,1,0:T(2,128)} %remote_ref.1, f32[12,275,275]{2,1,0:T(8,128)} %basis_hbm.1, f32[16,275]{1,0:T(8,128)} %load_ref.1, s32[6,16]{1,0:T(8,128)} %bitcast.6, ...), custom_call_target="tpu_custom_call" | custom-call | tf_op jit(solution)/shard_map/hdg/pallas_call | solution.py:530
  62.3 1.3 %slice_bitcast_fusion = (f32[25,64]{1,0:T(8,128)}, f32[25,64]{1,0:T(8,128)}) fusion(f32[2,32,128]{2,1,0:T(8,128)} %hdg.1), kind=kLoop, calls=%fused_computation | loop fusion | bytes 25600 | tf_op jit(solution)/shard_map/squeeze | solution.py:558
